TPU v7x, 32 devices: a whole 2x2x4 slice. The times are simulated.
32 devices in a mesh: seq: 16 (over z, y, x), head: 2 (over core).
Axes of the slice: x: 2, y: 2, z: 4, core: 2. Of those that a mesh axis runs over, the one named last changes fastest.
Arguments:
- queries: bfloat16 [4096, 4096], P('seq', 'head'), may hold values from -210 to 210
- keys: bfloat16 [4096, 1024], P('seq', 'head'), may hold values from -7 to 7
- values: bfloat16 [4096, 1024], P('seq', 'head'), may hold values from -6 to 6
- vertical: int32 [8, 16], P('head'), may hold values from 0 to 63, as said below
- slash: int32 [8, 2], P('head'), may hold values from 1 to 4, as said below
- out_weight: bfloat16 [4096, 4096], P('head'), may hold values from -1 to 1
Outputs:
- mixed: bfloat16 [4096, 4096], P(('seq', 'head'))
Inputs may be any that keep to these rules, and one draw needn't show every extreme that they name: `vertical`: for each key-value head, 16 different key blocks in increasing order; block b lies in slab b // 4; no slab holds more than 2 of one head's blocks, and for every head some slab holds exactly 2. `slash`: for each key-value head, 2 different offsets in increasing order; some head has the offset 256 // 64.
All inputs are finite; a program needn't handle non-finite values.
Results may differ from a plain program's by a relative error of at most 0.01.
Values may be sent and summed in bfloat16 or wider, within the bound.
A program may use at most 128 MiB of HBM per device.

v0:
```python
import math

import jax
import jax.numpy as jnp
from jax import lax
from jax.sharding import PartitionSpec as P

HEAD_DIM = 128
BLK = 64
CAP = 2


NEGATIVE = -1e30


def from_behind(shard, axis, by):
    peers = lax.axis_size(axis)
    pairs = [(i, i + by) for i in range(peers) if 0 <= i + by < peers]
    return lax.ppermute(shard, axis, pairs)


def spread(blockwise):
    return jnp.repeat(jnp.repeat(blockwise, BLK, axis=1), BLK, axis=2)


def attend(running, query_view, key_part, value_part, allowed):
    top_score, sum_weight, accumulated = running
    scores = jnp.einsum(
        "shgd,khd->hgsk", query_view, key_part, preferred_element_type=jnp.float32
    ) * HEAD_DIM ** (-0.5)
    scores = jnp.where(allowed[:, None], scores, NEGATIVE)
    new_top = jnp.maximum(top_score, jnp.max(scores, axis=-1))
    shrink = jnp.exp(top_score - new_top)
    weights = jnp.where(allowed[:, None], jnp.exp(scores - new_top[..., None]), 0.0)
    sum_weight = sum_weight * shrink + jnp.sum(weights, axis=-1)
    accumulated = accumulated * shrink[..., None] + jnp.einsum(
        "hgsk,khd->hgsd",
        weights.astype(jnp.bfloat16),
        value_part,
        preferred_element_type=jnp.float32,
    )
    return (new_top, sum_weight, accumulated)


def on_device(queries, keys, values, vertical, slash, out_weight):
    row_count = queries.shape[0]
    kv_local = vertical.shape[0]
    chosen_count = vertical.shape[1]
    per_group = queries.shape[1] // (kv_local * HEAD_DIM)
    slab_blocks = row_count // BLK
    my_slab = lax.axis_index("seq")
    first_block = my_slab * slab_blocks
    block_ids = first_block + jnp.arange(slab_blocks, dtype=jnp.int32)
    query_view = queries.reshape(row_count, kv_local, per_group, HEAD_DIM)
    key_view = keys.reshape(row_count, kv_local, HEAD_DIM)
    value_view = values.reshape(row_count, kv_local, HEAD_DIM)
    running = (
        jnp.full((kv_local, per_group, row_count), NEGATIVE, jnp.float32),
        jnp.zeros((kv_local, per_group, row_count), jnp.float32),
        jnp.zeros((kv_local, per_group, row_count, HEAD_DIM), jnp.float32),
    )

    def on_slash(distance):
        return jnp.any(slash[:, None, None, :] == distance[..., None], axis=-1)

    local_blocks = jnp.arange(slab_blocks, dtype=jnp.int32)
    block_gap = local_blocks[:, None] - local_blocks[None, :]
    prev_keys, prev_values = from_behind((keys, values), "seq", 1)
    prev_allowed = spread(on_slash(block_gap + slab_blocks) & (my_slab > 0))
    running = attend(
        running,
        query_view,
        prev_keys.reshape(row_count, kv_local, HEAD_DIM),
        prev_values.reshape(row_count, kv_local, HEAD_DIM),
        prev_allowed,
    )
    token_ids = jnp.arange(row_count)
    causal = token_ids[None, :] <= token_ids[:, None]
    same_block = jnp.broadcast_to(block_gap == 0, (kv_local, slab_blocks, slab_blocks))
    own_allowed = spread(on_slash(block_gap)) | spread(same_block) & causal[None]
    running = attend(running, query_view, key_view, value_view, own_allowed)
    holder_slab = vertical // slab_blocks
    earlier = jnp.arange(chosen_count)[None, :] < jnp.arange(chosen_count)[:, None]
    owner_rank = jnp.sum(
        (holder_slab[:, :, None] == holder_slab[:, None, :]) & earlier[None], axis=-1
    )

    def slot_table(slots):
        holder = slots // CAP
        slot_place = slots % CAP
        matches = (holder_slab[:, None, :] == holder[None, :, None]) & (
            owner_rank[:, None, :] == slot_place[None, :, None]
        )
        return (
            jnp.sum(jnp.where(matches, vertical[:, None, :], 0), axis=-1),
            jnp.any(matches, axis=-1),
        )

    key_blocks = keys.reshape(slab_blocks, BLK, kv_local, HEAD_DIM)
    value_blocks = values.reshape(slab_blocks, BLK, kv_local, HEAD_DIM)
    my_blocks, holding = slot_table(my_slab * CAP + jnp.arange(CAP, dtype=jnp.int32))
    picker = jnp.where(holding, my_blocks - first_block, 0).T[:, None, :, None]
    send_keys = jnp.take_along_axis(key_blocks, picker, axis=0)
    send_values = jnp.take_along_axis(value_blocks, picker, axis=0)
    pieces = (
        lax.all_gather(send_keys, "seq", axis=0, tiled=True),
        lax.all_gather(send_values, "seq", axis=0, tiled=True),
    )
    slot_amount = pieces[0].shape[0]
    slot_blocks, present = slot_table(jnp.arange(slot_amount, dtype=jnp.int32))
    current = running
    key_slots = pieces[0]
    value_slots = pieces[1]
    slot_total = key_slots.shape[0]
    group_slots = math.gcd(slot_total, 8)
    group_count = slot_total // group_slots
    key_groups = key_slots.reshape(group_count, group_slots * BLK, kv_local, HEAD_DIM)
    value_groups = value_slots.reshape(group_count, group_slots * BLK, kv_local, HEAD_DIM)
    block_groups = slot_blocks.reshape(kv_local, group_count, group_slots).transpose(1, 0, 2)
    present_groups = present.reshape(kv_local, group_count, group_slots).transpose(1, 0, 2)

    def advance(partial_state, pieces):
        key_group, value_group, block_group, present_group = pieces
        distance = block_ids[None, :, None] - block_group[:, None, :]
        usable = present_group[:, None, :] & (distance > 0) & jnp.logical_not(on_slash(distance))
        return (attend(partial_state, query_view, key_group, value_group, spread(usable)), None)

    current, unused = lax.scan(
        advance, current, (key_groups, value_groups, block_groups, present_groups)
    )
    running = current
    top_score, sum_weight, accumulated = running
    attention = (accumulated / sum_weight[..., None]).astype(jnp.bfloat16)
    attention = attention.transpose(2, 0, 1, 3).reshape(row_count, kv_local * per_group * HEAD_DIM)
    return lax.psum_scatter(
        jnp.dot(attention, out_weight, preferred_element_type=jnp.float32).astype(jnp.bfloat16),
        "head",
        scatter_dimension=0,
        tiled=True,
    )


def solution(mesh):
    placed = (
        P("seq", "head"),
        P("seq", "head"),
        P("seq", "head"),
        P("head", None),
        P("head", None),
        P("head", None),
    )
    return jax.shard_map(
        on_device, mesh=mesh, in_specs=placed, out_specs=P(("seq", "head"), None), check_vma=False
    )
```

profile of v0, /device:TPU:27, one launch (start us, length us, event | category | flops | bytes accessed | tf_op | source)
XLA Modules:
  0.0 208.8 jit_solution(6682734317268306873)
XLA Ops:
  6.6 0.8 add_select_fusion
  7.4 0.2 convert_reduce_fusion
  7.6 0.9 select_reduce_fusion.1
  8.5 0.1 reduce_or.48
  8.8 1.0 reshape.229
  9.8 1.0 reshape.231
  10.9 0.6 gather_fusion
  11.5 0.6 gather_fusion.1
  12.1 0.1 copy.92
  12.2 0.8 fusion.46
  13.1 1.8 copy.79
  14.9 3.1 %collective-permute-start = (bf16[256,512]{0,1:T(8,128)(2,1)}, bf16[256,512]{0,1:T(8,128)(2,1)}, u32[]{:S(2)}, u32[]{:S(2)}) collective-permute-start(bf16[256,512]{0,1:T(8,128)(2,1)} %copy.79), channel_id=1, source_target_pairs={{0,2},{2,4},{4,6},{6,8},{8,10},{10,12},{12,14},{14,16},{16,18},{18... | collective-permute-start | bytes 786440 | tf_op jit(solution)/shard_map/ppermute | solution.py:19
  18.0 1.8 copy.87
  19.8 3.1 %collective-permute-start.1 = (bf16[256,512]{0,1:T(8,128)(2,1)}, bf16[256,512]{0,1:T(8,128)(2,1)S(1)}, u32[]{:S(2)}, u32[]{:S(2)}) collective-permute-start(bf16[256,512]{0,1:T(8,128)(2,1)} %copy.87), channel_id=1, source_target_pairs={{0,2},{2,4},{4,6},{6,8},{8,10},{10,12},{12,14},{14,16},{16,18},{18... | collective-permute-start | bytes 786440 | tf_op jit(solution)/shard_map/ppermute | solution.py:19
  23.1 0.8 reshape.226
  24.0 0.1 copy.78
  24.3 0.5 copy.80
  24.9 0.1 copy.83
  25.2 0.1 copy.84
  25.5 0.1 select_reduce_fusion
  25.7 0.1 fusion.48
  25.9 0.7 copy.102
  26.6 0.1 bitcast_or_fusion
  26.7 0.9 fusion.21
  27.7 1.9 fusion.20
  29.7 1.1 fusion.25
  30.7 1.5 fusion.26
  32.2 1.1 fusion.23
  33.4 3.1 %multiply_add_fusion.2 = f32[4,4,256,128]{3,2,1,0:T(8,128)S(1)} fusion(f32[4,4,256,128]{3,2,1,0:T(8,128)S(1)} %fusion.26, bf16[256,4,128,1]{0,2,3,1:T(8,128)(2,1)S(1)} %bitcast.189, f32[4,256,256,4]{2,1,3,0:T(8,128)S(1)} %get-tuple-element.173, f32[4,4,256]{2,1,0:T(4,128)S(1)} %get-tuple-element.169, pred[4,256,256]{1,2,0:T(8,128)(4,1)S(1)} %bitcast.173, ...), kind=kOutput, calls=%fused_computation.43 | convolution fusion | flops 275251200 | bytes 8962048 | tf_op jit(solution)/shard_map/hgsk,khd->hgsd/dot_general | solution.py:36
  36.5 37.4 %all-gather.3.cloned.1.call-done = bf16[32,64,4,128]{3,1,0,2:T(8,128)(2,1)} async-done(((bf16[2,64,4,128]{3,1,0,2:T(8,128)(2,1)}), bf16[32,64,4,128]{3,1,0,2:T(8,128)(2,1)}) %all-gather.3.cloned.1.call-update) | async-done | bytes 2097168 | tf_op jit(solution)/shard_map/all_gather | solution.py:106
  73.9 62.5 %all-gather.5.cloned.1.call-done = bf16[32,64,4,128]{3,1,0,2:T(8,128)(2,1)} async-done(((bf16[2,64,4,128]{3,1,0,2:T(8,128)(2,1)}), bf16[32,64,4,128]{3,1,0,2:T(8,128)(2,1)}) %all-gather.5.cloned.1.call-update) | async-done | bytes 2097168 | tf_op jit(solution)/shard_map/all_gather | solution.py:107
  136.4 38.2 %while.15 = (s32[]{:T(128)}, f32[4,4,256]{2,1,0:T(4,128)S(1)}, f32[4,4,256]{2,1,0:T(4,128)S(1)}, f32[4,4,256,128]{3,2,1,0:T(8,128)S(1)}, pred[4,4,8]{2,1,0:T(4,1...) while((s32[]{:T(128)}, f32[4,4,256]{2,1,0:T(4,128)S(1)}, ...), condition=%wide.region_15.17_spmd.clone, body=%wide.region_11.16_spmd.clone.sunk | while | flops 1102062720 | bytes 33852976 | solution.py:128
  136.7 0.1 copy.140
  136.8 0.1 broadcast_in_dim.288
  136.9 0.1 reshape.275
  137.0 0.1 broadcast_in_dim.289
  137.2 2.5 %fusion.75 = (f32[4,4,256]{2,1,0:T(4,128)S(1)}, f32[4,512,256,4]{2,1,3,0:T(8,128)S(1)}) fusion(pred[4,256,512]{1,2,0:T(8,128)(4,1)S(1)} %bitcast.161, bf16[256,4,4,128]{3,0,2,1:T(8,128)(2,1)S(1)} %get-tuple-element.293, bf16[4,512,4,128]{3,1,0,2:T(8,128)(2,1)} %get-tuple-element.292, s32[]{:T(128)} %get-tuple-element.273), kind=kOutput, calls=%fused_computation.5.clone.1 | convolution fusion | flops 543158272 | bytes 10502656 | tf_op jit(solution)/shard_map/while/body/eval_jaxpr/shgd,khd->hgsk/dot_general | solution.py:28
  139.7 2.1 %fusion.76 = f32[4,4,256]{2,1,0:T(4,128)S(1)} fusion(f32[4,512,256,4]{2,1,3,0:T(8,128)S(1)} %get-tuple-element.258, f32[4,4,256]{2,1,0:T(4,128)S(1)} %max.20, pred[4,256,512]{1,2,0:T(8,128)(4,1)S(1)} %bitcast.162), kind=kLoop, calls=%fused_computation.7.clone.1 | loop fusion | flops 10481664 | bytes 8945664 | tf_op jit(solution)/shard_map/while/body/eval_jaxpr/reduce_sum | solution.py:35
  141.8 4.1 %multiply_add_fusion.7 = f32[4,4,256,128]{3,2,1,0:T(8,128)S(1)} fusion(f32[4,4,256,128]{3,2,1,0:T(8,128)S(1)} %get-tuple-element.276, f32[4,512,256,4]{2,1,3,0:T(8,128)S(1)} %get-tuple-element.258, f32[4,4,256]{2,1,0:T(4,128)S(1)} %max.20, pred[4,256,512]{1,2,0:T(8,128)(4,1)S(1)} %bitcast.163, f32[4,4,256]{2,1,0:T(4,128)S(1)} %bitcast.182, ...), kind=kOutput, calls=%fused_computation.10.clone.1 | convolution fusion | flops 548405248 | bytes 13664768 | tf_op jit(solution)/shard_map/while/body/eval_jaxpr/hgsk,khd->hgsd/dot_general | solution.py:36
  146.2 0.1 copy.140
  146.4 0.1 broadcast_in_dim.288
  146.5 0.1 reshape.275
  146.6 0.1 broadcast_in_dim.289
  146.7 2.5 %fusion.75 = (f32[4,4,256]{2,1,0:T(4,128)S(1)}, f32[4,512,256,4]{2,1,3,0:T(8,128)S(1)}) fusion(pred[4,256,512]{1,2,0:T(8,128)(4,1)S(1)} %bitcast.161, bf16[256,4,4,128]{3,0,2,1:T(8,128)(2,1)S(1)} %get-tuple-element.293, bf16[4,512,4,128]{3,1,0,2:T(8,128)(2,1)} %get-tuple-element.292, s32[]{:T(128)} %get-tuple-element.273), kind=kOutput, calls=%fused_computation.5.clone.1 | convolution fusion | flops 543158272 | bytes 10502656 | tf_op jit(solution)/shard_map/while/body/eval_jaxpr/shgd,khd->hgsk/dot_general | solution.py:28
  149.2 2.1 %fusion.76 = f32[4,4,256]{2,1,0:T(4,128)S(1)} fusion(f32[4,512,256,4]{2,1,3,0:T(8,128)S(1)} %get-tuple-element.258, f32[4,4,256]{2,1,0:T(4,128)S(1)} %max.20, pred[4,256,512]{1,2,0:T(8,128)(4,1)S(1)} %bitcast.162), kind=kLoop, calls=%fused_computation.7.clone.1 | loop fusion | flops 10481664 | bytes 8945664 | tf_op jit(solution)/shard_map/while/body/eval_jaxpr/reduce_sum | solution.py:35
  151.4 4.1 %multiply_add_fusion.7 = f32[4,4,256,128]{3,2,1,0:T(8,128)S(1)} fusion(f32[4,4,256,128]{3,2,1,0:T(8,128)S(1)} %get-tuple-element.276, f32[4,512,256,4]{2,1,3,0:T(8,128)S(1)} %get-tuple-element.258, f32[4,4,256]{2,1,0:T(4,128)S(1)} %max.20, pred[4,256,512]{1,2,0:T(8,128)(4,1)S(1)} %bitcast.163, f32[4,4,256]{2,1,0:T(4,128)S(1)} %bitcast.182, ...), kind=kOutput, calls=%fused_computation.10.clone.1 | convolution fusion | flops 548405248 | bytes 13664768 | tf_op jit(solution)/shard_map/while/body/eval_jaxpr/hgsk,khd->hgsd/dot_general | solution.py:36
  155.8 0.1 copy.140
  155.9 0.1 broadcast_in_dim.288
  156.1 0.1 broadcast_in_dim.289
  156.3 2.5 %fusion.75 = (f32[4,4,256]{2,1,0:T(4,128)S(1)}, f32[4,512,256,4]{2,1,3,0:T(8,128)S(1)}) fusion(pred[4,256,512]{1,2,0:T(8,128)(4,1)S(1)} %bitcast.161, bf16[256,4,4,128]{3,0,2,1:T(8,128)(2,1)S(1)} %get-tuple-element.293, bf16[4,512,4,128]{3,1,0,2:T(8,128)(2,1)} %get-tuple-element.292, s32[]{:T(128)} %get-tuple-element.273), kind=kOutput, calls=%fused_computation.5.clone.1 | convolution fusion | flops 543158272 | bytes 10502656 | tf_op jit(solution)/shard_map/while/body/eval_jaxpr/shgd,khd->hgsk/dot_general | solution.py:28
  158.8 2.1 %fusion.76 = f32[4,4,256]{2,1,0:T(4,128)S(1)} fusion(f32[4,512,256,4]{2,1,3,0:T(8,128)S(1)} %get-tuple-element.258, f32[4,4,256]{2,1,0:T(4,128)S(1)} %max.20, pred[4,256,512]{1,2,0:T(8,128)(4,1)S(1)} %bitcast.162), kind=kLoop, calls=%fused_computation.7.clone.1 | loop fusion | flops 10481664 | bytes 8945664 | tf_op jit(solution)/shard_map/while/body/eval_jaxpr/reduce_sum | solution.py:35
  160.9 4.1 %multiply_add_fusion.7 = f32[4,4,256,128]{3,2,1,0:T(8,128)S(1)} fusion(f32[4,4,256,128]{3,2,1,0:T(8,128)S(1)} %get-tuple-element.276, f32[4,512,256,4]{2,1,3,0:T(8,128)S(1)} %get-tuple-element.258, f32[4,4,256]{2,1,0:T(4,128)S(1)} %max.20, pred[4,256,512]{1,2,0:T(8,128)(4,1)S(1)} %bitcast.163, f32[4,4,256]{2,1,0:T(4,128)S(1)} %bitcast.182, ...), kind=kOutput, calls=%fused_computation.10.clone.1 | convolution fusion | flops 548405248 | bytes 13664768 | tf_op jit(solution)/shard_map/while/body/eval_jaxpr/hgsk,khd->hgsd/dot_general | solution.py:36
  165.3 0.1 copy.140
  165.5 0.1 broadcast_in_dim.288
  165.6 0.1 reshape.275
  165.7 0.1 broadcast_in_dim.289
  165.8 2.5 %fusion.75 = (f32[4,4,256]{2,1,0:T(4,128)S(1)}, f32[4,512,256,4]{2,1,3,0:T(8,128)S(1)}) fusion(pred[4,256,512]{1,2,0:T(8,128)(4,1)S(1)} %bitcast.161, bf16[256,4,4,128]{3,0,2,1:T(8,128)(2,1)S(1)} %get-tuple-element.293, bf16[4,512,4,128]{3,1,0,2:T(8,128)(2,1)} %get-tuple-element.292, s32[]{:T(128)} %get-tuple-element.273), kind=kOutput, calls=%fused_computation.5.clone.1 | convolution fusion | flops 543158272 | bytes 10502656 | tf_op jit(solution)/shard_map/while/body/eval_jaxpr/shgd,khd->hgsk/dot_general | solution.py:28
  168.3 2.1 %fusion.76 = f32[4,4,256]{2,1,0:T(4,128)S(1)} fusion(f32[4,512,256,4]{2,1,3,0:T(8,128)S(1)} %get-tuple-element.258, f32[4,4,256]{2,1,0:T(4,128)S(1)} %max.20, pred[4,256,512]{1,2,0:T(8,128)(4,1)S(1)} %bitcast.162), kind=kLoop, calls=%fused_computation.7.clone.1 | loop fusion | flops 10481664 | bytes 8945664 | tf_op jit(solution)/shard_map/while/body/eval_jaxpr/reduce_sum | solution.py:35
  170.5 4.1 %multiply_add_fusion.7 = f32[4,4,256,128]{3,2,1,0:T(8,128)S(1)} fusion(f32[4,4,256,128]{3,2,1,0:T(8,128)S(1)} %get-tuple-element.276, f32[4,512,256,4]{2,1,3,0:T(8,128)S(1)} %get-tuple-element.258, f32[4,4,256]{2,1,0:T(4,128)S(1)} %max.20, pred[4,256,512]{1,2,0:T(8,128)(4,1)S(1)} %bitcast.163, f32[4,4,256]{2,1,0:T(4,128)S(1)} %bitcast.182, ...), kind=kOutput, calls=%fused_computation.10.clone.1 | convolution fusion | flops 548405248 | bytes 13664768 | tf_op jit(solution)/shard_map/while/body/eval_jaxpr/hgsk,khd->hgsd/dot_general | solution.py:36
  174.6 1.3 copy-done.2
  176.0 1.9 copy.104
  177.9 0.2 divide_convert_fusion
  178.1 11.8 %convolution_convert_fusion = bf16[256,4096]{1,0:T(8,128)(2,1)} fusion(bf16[256,2048]{0,1:T(8,128)(2,1)S(1)} %bitcast.168, bf16[2048,4096]{1,0:T(8,128)(2,1)} %param.15), kind=kOutput, calls=%fused_computation.29 | convolution fusion | flops 4296015872 | bytes 19922944 | tf_op jit(solution)/shard_map/dot_general | solution.py:136
  189.9 12.4 %reduce-scatter.2.cloned.1.call-done = bf16[128,4096]{1,0:T(8,128)(2,1)} async-done(((bf16[256,4096]{1,0:T(8,128)(2,1)}), bf16[128,4096]{1,0:T(8,128)(2,1)}) %reduce-scatter.2.cloned.1.call-update) | async-done | bytes 1048592 | tf_op jit(solution)/shard_map/reduce_scatter | solution.py:135
  (85 shorter events, 2.8 us)
Async XLA Ops:
  6.5 19.0 %copy-start.5 = (s32[4,16]{1,0:T(4,128)S(1)}, s32[4,16]{1,0:T(4,128)}, u32[]{:S(2)}) copy-start(s32[4,16]{1,0:T(4,128)} %param.13) | copy-start | bytes 772
  6.5 16.4 %copy-start = (bf16[256,512]{1,0:T(8,128)(2,1)S(1)}, bf16[256,512]{1,0:T(8,128)(2,1)}, u32[]{:S(2)}) copy-start(bf16[256,512]{1,0:T(8,128)(2,1)} %param.11) | copy-start | bytes 786436
  6.5 16.5 %copy-start.1 = (bf16[256,512]{1,0:T(8,128)(2,1)S(1)}, bf16[256,512]{1,0:T(8,128)(2,1)}, u32[]{:S(2)}) copy-start(bf16[256,512]{1,0:T(8,128)(2,1)} %param.12) | copy-start | bytes 786436
  6.5 17.3 %copy-start.6 = (s32[4,2]{0,1:T(2,128)S(1)}, s32[4,2]{0,1:T(2,128)}, u32[]{:S(2)}) copy-start(s32[4,2]{0,1:T(2,128)} %param.14) | copy-start | bytes 100
  6.5 17.8 %copy-start.3 = (bf16[256,2048]{1,0:T(8,128)(2,1)S(1)}, bf16[256,2048]{1,0:T(8,128)(2,1)}, u32[]{:S(2)}) copy-start(bf16[256,2048]{1,0:T(8,128)(2,1)} %param.10) | copy-start | bytes 3145732
  6.5 67.4 %all-gather.3.cloned.1.call-start = ((), (), s32[]{:S(2)}) async-start(), calls=%async_computation.1 | async-start | bytes 2228224 | tf_op jit(solution)/shard_map/all_gather | solution.py:106
  13.0 123.4 %all-gather.5.cloned.1.call-start = ((), (), s32[]{:S(2)}) async-start(), calls=%async_computation.2 | async-start | bytes 2228224 | tf_op jit(solution)/shard_map/all_gather | solution.py:107
  14.9 12.8 %collective-permute-start = (bf16[256,512]{0,1:T(8,128)(2,1)}, bf16[256,512]{0,1:T(8,128)(2,1)}, u32[]{:S(2)}, u32[]{:S(2)}) collective-permute-start(bf16[256,512]{0,1:T(8,128)(2,1)} %copy.79), channel_id=1, source_target_pairs={{0,2},{2,4},{4,6},{6,8},{8,10},{10,12},{12,14},{14,16},{16,18},{18... | collective-permute-start | bytes 786440 | tf_op jit(solution)/shard_map/ppermute | solution.py:19
  19.8 13.6 %collective-permute-start.1 = (bf16[256,512]{0,1:T(8,128)(2,1)}, bf16[256,512]{0,1:T(8,128)(2,1)S(1)}, u32[]{:S(2)}, u32[]{:S(2)}) collective-permute-start(bf16[256,512]{0,1:T(8,128)(2,1)} %copy.87), channel_id=1, source_target_pairs={{0,2},{2,4},{4,6},{6,8},{8,10},{10,12},{12,14},{14,16},{16,18},{18... | collective-permute-start | bytes 786440 | tf_op jit(solution)/shard_map/ppermute | solution.py:19
  22.9 179.4 %reduce-scatter.2.cloned.1.call-start = ((), (), s32[]{:S(2)}) async-start(), calls=%async_computation.3 | async-start | bytes 3145728 | tf_op jit(solution)/shard_map/reduce_scatter | solution.py:135
  27.7 3.0 %copy-start.4 = (bf16[256,4,128]{2,1,0:T(4,128)(2,1)S(1)}, bf16[256,4,128]{2,1,0:T(4,128)(2,1)}, u32[]{:S(2)}) copy-start(bf16[256,4,128]{2,1,0:T(4,128)(2,1)} %reshape.226) | copy-start | bytes 786436
  174.6 1.4 copy-start.2
Sparse Core Ops, SparseCore 0:
  13.1 60.7 all-gather.2
  76.7 59.6 all-gather.4
  190.0 12.2 reduce-scatter.1
where the time goes:
time: 211 us; the launch traced here: 209 us
  waiting for transfers between devices  112 us (53%)
  matrix products  45.6 us (22%)
  local copies, waits for them, and re-layouts  15.5 us (7%)
  other arithmetic  15.2 us (7%)
  between operations  13.4 us (6%)
  starting transfers between devices  6.34 us (3%)
    all_gather x1, waiting for transfers between devices, on_device(): lax.all_gather(send_values, 'seq', axis=0, tiled=True)  62.5 us
    all_gather x1, waiting for transfers between devices, on_device(): lax.all_gather(send_keys, 'seq', axis=0, tiled=True)  37.4 us
    dot_general x6, matrix products, attend(): jnp.einsum('hgsk,khd->hgsd', weights.astype(jnp.bfloat16), value_part, pr...  21.1 us
    dot_general x6, matrix products, attend(): jnp.einsum('shgd,khd->hgsk', query_view, key_part, preferred_element_type...  12.8 us
    reduce_scatter x1, waiting for transfers between devices, on_device(): lax.psum_scatter(jnp.dot(attention, out_weight, preferred_element_type=jn...  12.4 us
    dot_general x1, matrix products, on_device(): jnp.dot(attention, out_weight, preferred_element_type=jnp.float32)  11.8 us
    reduce_sum x6, other arithmetic, attend(): sum_weight = sum_weight * shrink + jnp.sum(weights, axis=-1)  10.6 us
    unnamed x20, local copies, waits for them, and re-layouts  6.22 us
  transfers between devices with their start and end apart: 5, of which 3 were waited for; matrix products, arithmetic and copies ran while one was open for 8% of the time, Pallas kernels for 0%

commit v1 on v0

v1 whole, which is shorter than its diff:
```python
import functools
import math

import jax
import jax.numpy as jnp
from jax import lax
from jax.experimental import pallas as pl
from jax.experimental.pallas import tpu as pltpu
from jax.sharding import PartitionSpec as P

HEAD_DIM = 128
BLK = 64
CAP = 2
NEGATIVE = -1e30
MESH = pl.DeviceIdType.MESH
SCALE = HEAD_DIM ** (-0.5) * math.log2(math.e)


def kernel(
    n, inner, kv, per_group, tile,
    q_ref, k_ref, v_ref, pack_ref, bias_ref, w_hbm, out_ref,
    slots, prev, w_ref, acc, top, total, attn, res, give, take,
    w_sem, prev_send, prev_recv, slot_recv, k_out, k_in, k_fwd, v_in, v_out, x_send, x_recv,
):
    rows = q_ref.shape[0]
    outer = n // inner
    me = lax.axis_index("seq")
    core = lax.axis_index("head")
    o, c = me // inner, me % inner
    other = 1 - core
    slab_blocks = rows // BLK
    half = rows // 2
    slot_keys = CAP * BLK

    barrier = pltpu.get_barrier_semaphore()

    def greet(seq, head):
        pl.semaphore_signal(barrier, inc=1, device_id=(seq, head), device_id_type=MESH)

    greet(me, other)
    for d in range(1, inner):
        greet(o * inner + (c + d) % inner, core)
    for d in range(1, outer):
        greet(((o + d) % outer) * inner + c, core)

    @pl.when(me + 1 < n)
    def _():
        greet(me + 1, core)

    @pl.when(me > 0)
    def _():
        greet(me - 1, core)

    weight_copy = pltpu.make_async_copy(w_hbm, w_ref, w_sem)
    weight_copy.start()
    pl.semaphore_wait(
        barrier,
        1 + (inner - 1) + (outer - 1) + jnp.where(me > 0, 1, 0) + jnp.where(me + 1 < n, 1, 0),
    )

    sends = []

    def remote(src, dst, send_sem, recv_sem, seq):
        return pltpu.make_async_remote_copy(
            src_ref=src, dst_ref=dst, send_sem=send_sem, recv_sem=recv_sem,
            device_id=(seq, core), device_id_type=MESH,
        )

    def launch(cond, *args):
        def begin():
            remote(*args).start()

        pl.when(cond)(begin)
        sends.append((cond, args))

    def arrived(slab, part):
        remote(slots.at[slab, part], slots.at[slab, part], k_out.at[0],
               slot_recv.at[slab, part], (me + 1) % n).wait_recv()

    for d in range(1, outer):
        launch(o + d < outer, pack_ref.at[0], slots.at[me, 0], k_out.at[d], slot_recv.at[me, 0],
               me + d * inner)
    for d in range(1, inner):
        peer = (c + d) % inner
        launch((o < outer - 1) | (peer > c), pack_ref.at[1], slots.at[me, 1], v_in.at[d],
               slot_recv.at[me, 1], o * inner + peer)
    for d in range(1, inner):
        peer = (c + d) % inner
        launch(peer > c, pack_ref.at[0], slots.at[me, 0], k_in.at[d], slot_recv.at[me, 0],
               o * inner + peer)
    for d in range(1, outer):
        launch(o + d < outer, pack_ref.at[1], slots.at[me, 1], v_out.at[0, d], slot_recv.at[me, 1],
               me + d * inner)
    launch(me + 1 < n, k_ref, prev.at[0], prev_send.at[0], prev_recv.at[0], me + 1)
    launch(me + 1 < n, v_ref, prev.at[1], prev_send.at[1], prev_recv.at[1], me + 1)

    def attend(get_k, get_v, bias_row, causal):
        def one_head(h, _):
            k = get_k(h)
            vt = get_v(h).T
            pieces = k.shape[0] // BLK
            for g in range(per_group):
                j = h * per_group + g
                q = q_ref[:, pl.ds(pl.multiple_of(j * HEAD_DIM, HEAD_DIM), HEAD_DIM)]
                s = lax.dot_general(k, q, (((1,), (1,)), ((), ())),
                                    preferred_element_type=jnp.float32) * SCALE
                parts = [
                    s[i * BLK:(i + 1) * BLK] + bias_ref[h, pl.ds(bias_row + i, 1), :]
                    for i in range(pieces)
                ]
                s = jnp.concatenate(parts, axis=0)
                if causal:
                    keys_at = lax.broadcasted_iota(jnp.int32, s.shape, 0)
                    query_at = lax.broadcasted_iota(jnp.int32, s.shape, 1)
                    s = jnp.where(keys_at <= query_at, s, NEGATIVE)
                peak = jnp.max(s, axis=0, keepdims=True)
                if causal:
                    p = jnp.exp2(s - peak)
                    top[j] = peak
                    total[j] = jnp.sum(p, axis=0, keepdims=True)
                    acc[j] = jnp.dot(vt, p.astype(jnp.bfloat16), preferred_element_type=jnp.float32)
                else:
                    before = top[j]
                    peak = jnp.maximum(before, peak)
                    shrink = jnp.exp2(before - peak)
                    p = jnp.exp2(s - peak)
                    top[j] = peak
                    total[j] = total[j] * shrink + jnp.sum(p, axis=0, keepdims=True)
                    acc[j] = acc[j] * shrink + jnp.dot(
                        vt, p.astype(jnp.bfloat16), preferred_element_type=jnp.float32)
            return 0

        lax.fori_loop(0, kv, one_head, 0)

    def lanes(h):
        return pl.ds(pl.multiple_of(h * HEAD_DIM, HEAD_DIM), HEAD_DIM)

    def attend_slots(slab, count):
        def get(part):
            return lambda h: jnp.concatenate(
                [slots[slab + i, part, :, lanes(h)] for i in range(count)], axis=0)

        attend(get(0), get(1), 2 * slab_blocks + slab * CAP, False)

    attend(lambda h: k_ref[:, lanes(h)], lambda h: v_ref[:, lanes(h)], 0, True)

    for d in range(1, max(inner, outer)):
        if d < outer:
            source = me - d * inner

            @pl.when(d <= o)
            def _(source=source):
                arrived(source, 0)

            for e in range(1, inner):
                launch(d <= o, slots.at[source, 0], slots.at[source, 0], k_fwd.at[d, e],
                       slot_recv.at[source, 0], o * inner + (c + e) % inner)
        if d < inner:
            peer = (c + inner - d) % inner
            source = o * inner + peer

            @pl.when((o < outer - 1) | (peer < c))
            def _(source=source):
                arrived(source, 1)

            for e in range(1, outer):
                launch(o + e < outer, slots.at[source, 1], slots.at[source, 1], v_out.at[d, e],
                       slot_recv.at[source, 1], me + e * inner)

    for near in range(inner - 1):
        @pl.when(near < c)
        def _(near=near):
            arrived(o * inner + near, 0)
            attend_slots(o * inner + near, 1)

    @pl.when(me > 0)
    def _():
        for i in range(2):
            remote(prev.at[i], prev.at[i], prev_send.at[i], prev_recv.at[i], (me + 1) % n).wait_recv()
        attend(lambda h: prev[0, :, lanes(h)], lambda h: prev[1, :, lanes(h)], slab_blocks, False)

    step = 2 if inner % 2 == 0 else 1

    def plane(d, _):
        base = (o - 1 - d) * inner
        for part in range(0, inner, step):
            for i in range(part, part + step):
                @pl.when(c != i)
                def _(i=i):
                    arrived(base + i, 0)

                arrived(base + i, 1)
            attend_slots(base + part, step)
        return 0

    lax.fori_loop(0, o, plane, 0)

    def finish(j, _):
        a = acc[j] / total[j]
        attn[:, lanes(j)] = a.T.astype(jnp.bfloat16)
        return 0

    lax.fori_loop(0, kv * per_group, finish, 0)
    weight_copy.wait()
    tiles = give.shape[0]
    mine = pl.ds(pl.multiple_of(core * half, half), half)
    theirs = pl.ds(pl.multiple_of(other * half, half), half)

    def swap(t):
        return pltpu.make_async_remote_copy(
            src_ref=give.at[t], dst_ref=take.at[t], send_sem=x_send.at[t], recv_sem=x_recv.at[t],
            device_id=(me, other), device_id_type=MESH,
        )

    def project(t, _):
        columns = pl.ds(pl.multiple_of(t * tile, tile), tile)
        res[t] = jnp.dot(attn[...], w_ref[:, columns], preferred_element_type=jnp.float32)
        give[t] = res[t, theirs, :].astype(jnp.bfloat16)
        swap(t).start()
        return 0

    lax.fori_loop(0, tiles, project, 0)

    def add_up(t, _):
        columns = pl.ds(pl.multiple_of(t * tile, tile), tile)
        swap(t).wait_recv()
        out_ref[:, columns] = (res[t, mine, :] + take[t].astype(jnp.float32)).astype(out_ref.dtype)
        return 0

    lax.fori_loop(0, tiles, add_up, 0)

    def sent(t, _):
        swap(t).wait_send()
        return 0

    lax.fori_loop(0, tiles, sent, 0)
    for cond, args in sends:
        def settle(args=args):
            remote(*args).wait_send()

        pl.when(cond)(settle)


def on_device(n, queries, keys, values, vertical, slash, out_weight):
    rows = queries.shape[0]
    kv = vertical.shape[0]
    per_group = queries.shape[1] // (kv * HEAD_DIM)
    slab_blocks = rows // BLK
    inner = math.gcd(n, 4)
    outer = n // inner
    model = out_weight.shape[1]
    my_slab = lax.axis_index("seq")
    first_block = my_slab * slab_blocks

    slab_ids = jnp.arange(n, dtype=jnp.int32)
    held_by = (vertical // slab_blocks)[:, None, :] == slab_ids[None, :, None]
    none = n * slab_blocks
    low = jnp.min(jnp.where(held_by, vertical[:, None, :], none), axis=-1)
    high = jnp.max(jnp.where(held_by, vertical[:, None, :], -1), axis=-1)
    slot_block = jnp.stack([low, jnp.where(high > low, high, none)], axis=-1).reshape(kv, n * CAP)
    local = jnp.arange(slab_blocks, dtype=jnp.int32)
    key_block = jnp.concatenate(
        [
            jnp.broadcast_to((first_block + local)[None], (kv, slab_blocks)),
            jnp.broadcast_to((first_block - slab_blocks + local)[None], (kv, slab_blocks)),
            slot_block,
        ],
        axis=1,
    )
    query_block = first_block + jnp.arange(rows, dtype=jnp.int32) // BLK
    gap = query_block[None, None, :] - key_block[:, :, None]
    on_slash = jnp.any(gap[..., None] == slash[:, None, None, :], axis=-1)
    row_ids = jnp.arange(key_block.shape[1])[None, :, None]
    chosen = jnp.any(key_block[:, :, None] == vertical[:, None, :], axis=-1)[:, :, None]
    later = gap > 0
    allowed = jnp.where(
        row_ids < slab_blocks,
        on_slash | (gap == 0) | (chosen & later),
        jnp.where(row_ids < 2 * slab_blocks, on_slash & (my_slab > 0), later & ~on_slash),
    )
    bias = jnp.where(allowed, 0.0, NEGATIVE).astype(jnp.float32)

    inside = (vertical // slab_blocks) == my_slab
    my_low = jnp.min(jnp.where(inside, vertical, none), axis=-1) - first_block
    my_high = jnp.max(jnp.where(inside, vertical, -1), axis=-1) - first_block
    pick = jnp.stack([my_low, my_high])
    pick = jnp.repeat(pick, HEAD_DIM, axis=1)[:, None, :]

    def packed(array):
        blocks = array.reshape(slab_blocks, BLK, kv * HEAD_DIM)
        chosen = jnp.broadcast_to(blocks[0][None], (CAP, BLK, kv * HEAD_DIM))
        for i in range(1, slab_blocks):
            chosen = jnp.where(pick == i, blocks[i][None], chosen)
        return chosen.reshape(CAP * BLK, kv * HEAD_DIM)

    pack = jnp.stack([packed(keys), packed(values)])

    tile = math.gcd(model, 512)
    tiles = model // tile
    heads = kv * per_group
    vmem = pl.BlockSpec(memory_space=pltpu.VMEM)
    dma = pltpu.SemaphoreType.DMA
    return pl.pallas_call(
        functools.partial(kernel, n, inner, kv, per_group, tile),
        out_shape=jax.ShapeDtypeStruct((rows // 2, model), jnp.bfloat16),
        in_specs=[vmem] * 5 + [pl.BlockSpec(memory_space=pl.ANY)],
        out_specs=vmem,
        scratch_shapes=[
            pltpu.VMEM((n, 2, CAP * BLK, kv * HEAD_DIM), jnp.bfloat16),
            pltpu.VMEM((2, rows, kv * HEAD_DIM), jnp.bfloat16),
            pltpu.VMEM(out_weight.shape, jnp.bfloat16),
            pltpu.VMEM((heads, HEAD_DIM, rows), jnp.float32),
            pltpu.VMEM((heads, 1, rows), jnp.float32),
            pltpu.VMEM((heads, 1, rows), jnp.float32),
            pltpu.VMEM((rows, heads * HEAD_DIM), jnp.bfloat16),
            pltpu.VMEM((tiles, rows, tile), jnp.float32),
            pltpu.VMEM((tiles, rows // 2, tile), jnp.bfloat16),
            pltpu.VMEM((tiles, rows // 2, tile), jnp.bfloat16),
            dma,
            dma((2,)),
            dma((2,)),
            dma((n, 2)),
            dma((outer,)),
            dma((inner,)),
            dma((outer, inner)),
            dma((inner,)),
            dma((inner, outer)),
            dma((tiles,)),
            dma((tiles,)),
        ],
        compiler_params=pltpu.CompilerParams(
            collective_id=0, has_side_effects=True, vmem_limit_bytes=60 * 2**20
        ),
    )(queries, keys, values, pack, bias, out_weight)


def solution(mesh):
    placed = (
        P("seq", "head"),
        P("seq", "head"),
        P("seq", "head"),
        P("head", None),
        P("head", None),
        P("head", None),
    )
    return jax.shard_map(
        functools.partial(on_device, mesh.shape["seq"]),
        mesh=mesh, in_specs=placed, out_specs=P(("seq", "head"), None), check_vma=False,
    )
```

time: 211 us -> 114 us (0.54)
  the two profiles are of different devices: /device:TPU:27 before, /device:TPU:31 now
where the time goes in v1:
time: 114 us; the launch traced here: 113 us
  Pallas kernels  104 us (91%)
  other arithmetic  5.24 us (5%)
  local copies, waits for them, and re-layouts  4.57 us (4%)
    pallas_call x1, Pallas kernels, on_device(): pl.pallas_call(functools.partial(kernel, n, inner, kv, per_group, tile),...  104 us
    unnamed x8, local copies, waits for them, and re-layouts  3.3 us

profile of v1, /device:TPU:31, one launch (start us, length us, event | category | flops | bytes accessed | tf_op | source)
XLA Modules:
  0.0 113.5 jit_solution(11209294566263168179)
XLA Ops:
  0.0 0.1 pad_add_fusion.3
  0.1 0.8 copy.16
  0.9 0.7 broadcast_compare_fusion
  1.6 0.8 select_reduce_fusion.3
  2.4 0.1 broadcast_bitcast_fusion.2
  2.5 0.1 broadcast_bitcast_fusion.1
  2.6 0.1 broadcast_bitcast_fusion
  2.7 0.9 select_reduce_fusion.1
  3.6 0.1 copy.14
  3.7 0.1 copy.15
  3.8 0.1 pad_add_fusion.1
  3.8 0.8 compare_reduce_fusion.1
  4.6 0.1 broadcast_subtract_fusion
  4.7 0.1 compare_reduce_fusion
  4.8 0.9 select_select_fusion.bias_ref
  5.7 1.1 fusion.3
  6.8 0.1 select_select_fusion.2
  6.9 0.7 pad_maximum_fusion.pack_ref
  7.6 103.6 %shard_map.64 = bf16[128,4096]{1,0:T(8,128)(2,1)} custom-call(bf16[256,2048]{1,0:T(8,128)(2,1)} %q_ref.1, bf16[256,512]{1,0:T(8,128)(2,1)} %k_ref.1, bf16[256,512]{1,0:T(8,128)(2,1)} %v_ref.1, bf16[2,128,512]{2,1,0:T(8,128)(2,1)} %pad_maximum_fusion.pack_ref, f32[4,40,256]{2,1,0:T(8,128)} %select_select_fusion.bias_ref, bf16[2048,4096]{1,0:T(8,128)(2,1)} %w_hbm.1), custom_call_target="tpu_custom_call" | custom-call | tf_op jit(solution)/shard_map/pallas_call | solution.py:303
  111.2 2.3 %copy.27 = bf16[128,4096]{1,0:T(8,128)(2,1)} copy(bf16[128,4096]{1,0:T(8,128)(2,1)} %shard_map.64) | data formatting | bytes 2097152
  (10 shorter events, 0.1 us)

commit v2 on v1

v2 whole, which is shorter than its diff:
```python
import functools
import math

import jax
import jax.numpy as jnp
from jax import lax
from jax.experimental import pallas as pl
from jax.experimental.pallas import tpu as pltpu
from jax.sharding import PartitionSpec as P

HEAD_DIM = 128
BLK = 64
CAP = 2
NEGATIVE = -1e30
MESH = pl.DeviceIdType.MESH
SCALE = HEAD_DIM ** (-0.5) * math.log2(math.e)


def kernel(
    n, inner, cut, kv, per_group, tile,
    q_ref, k_ref, v_ref, vert_ref, slash_ref, w_hbm, out_ref,
    pack_ref, bias_ref, slots, prev, w_ref, acc, top, total, attn, res, give, take,
    w_sem, prev_send, prev_recv, slot_recv, k_up, k_in, v_in, v_up, x_send, x_recv,
):
    rows = q_ref.shape[0]
    outer = n // inner
    me = lax.axis_index("seq")
    core = lax.axis_index("head")
    o, c = me // inner, me % inner
    other = 1 - core
    slab_blocks = rows // BLK
    half = rows // 2
    slot_keys = CAP * BLK

    barrier = pltpu.get_barrier_semaphore()

    def greet(seq, head):
        pl.semaphore_signal(barrier, inc=1, device_id=(seq, head), device_id_type=MESH)

    greet(me, other)
    for d in range(1, inner):
        greet(o * inner + (c + d) % inner, core)
    if outer > 1:
        greet((me + inner) % n, core)
        greet((me + n - inner) % n, core)

    @pl.when(me + 1 < n)
    def _():
        greet(me + 1, core)

    @pl.when(me > 0)
    def _():
        greet(me - 1, core)

    first_block = me * slab_blocks
    none = n * slab_blocks
    chosen_count = vert_ref.shape[1]
    for h in range(kv):
        low, high = jnp.int32(none), jnp.int32(-1)
        for i in range(chosen_count):
            block = vert_ref[h, i] - first_block
            inside = (block >= 0) & (block < slab_blocks)
            low = jnp.where(inside, jnp.minimum(low, block), low)
            high = jnp.where(inside, jnp.maximum(high, block), high)
        columns = slice(h * HEAD_DIM, (h + 1) * HEAD_DIM)
        for part, source in enumerate((k_ref, v_ref)):
            for slot, pick in enumerate((low, high)):
                got = source[:BLK, columns]
                for i in range(1, slab_blocks):
                    got = jnp.where(pick == i, source[i * BLK:(i + 1) * BLK, columns], got)
                at = part * slot_keys + slot * BLK
                pack_ref[at:at + BLK, columns] = got

    weight_copy = pltpu.make_async_copy(w_hbm, w_ref, w_sem)
    weight_copy.start()
    pl.semaphore_wait(
        barrier,
        1 + (inner - 1) + (2 if outer > 1 else 0) + jnp.where(me > 0, 1, 0) + jnp.where(me + 1 < n, 1, 0),
    )

    def remote(src, dst, send_sem, recv_sem, seq):
        return pltpu.make_async_remote_copy(
            src_ref=src, dst_ref=dst, send_sem=send_sem, recv_sem=recv_sem,
            device_id=(seq, core), device_id_type=MESH,
        )

    parts = (pl.ds(0, cut), pl.ds(cut, 2 * slot_keys - cut))
    above = (me + inner) % n

    def relay(slab, part, send_sem, seq, own=False):
        there = slots.at[slab, parts[part]]
        return remote(pack_ref.at[parts[part]] if own else there, there, send_sem,
                      slot_recv.at[slab, part], seq)

    def arrived(slab, part):
        relay(slab, part, k_up.at[0], above).wait_recv()

    def own_plane(act):
        for d in range(1, inner):
            peer = (c + d) % inner

            @pl.when((o < outer - 1) | (peer > c))
            def _(d=d, peer=peer):
                act(relay(me, 1, v_in.at[d], o * inner + peer, own=True))

        @pl.when(o < outer - 1)
        def _():
            act(relay(me, 0, k_up.at[0], above, own=True))

        for d in range(1, inner):
            peer = (c + d) % inner

            @pl.when(peer > c)
            def _(d=d, peer=peer):
                act(relay(me, 0, k_in.at[0, d], o * inner + peer, own=True))

        @pl.when(o < outer - 1)
        def _():
            act(relay(me, 1, v_up.at[0, 0], above, own=True))

        @pl.when(me + 1 < n)
        def _():
            for i, own in enumerate((k_ref, v_ref)):
                act(remote(own, prev.at[i], prev_send.at[i], prev_recv.at[i], me + 1))

    def spread_plane(d, start):
        act = (lambda copy: copy.start()) if start else (lambda copy: copy.wait_send())
        source = me - d * inner
        if start:
            arrived(source, 0)

        @pl.when(o < outer - 1)
        def _():
            act(relay(source, 0, k_up.at[d], above))

        for e in range(1, inner):
            act(relay(source, 0, k_in.at[d, e], o * inner + (c + e) % inner))
        for e in range(inner):
            slab = (o - d) * inner + (c + inner - e) % inner
            if start:
                arrived(slab, 1)

            @pl.when(o < outer - 1)
            def _(slab=slab, e=e):
                act(relay(slab, 1, v_up.at[d, e], above))

    own_plane(lambda copy: copy.start())

    def mask_rows(h, _):
        def filled(shape, value):
            return jnp.full(shape, value, jnp.int32)

        def on_slash(gap):
            hit = gap == slash_ref[h, 0]
            for i in range(1, slash_ref.shape[1]):
                hit = hit | (gap == slash_ref[h, i])
            return hit

        shape = (2 * slab_blocks, rows)
        row = lax.broadcasted_iota(jnp.int32, shape, 0)
        query_block = first_block + lax.broadcasted_iota(jnp.int32, shape, 1) // BLK
        block = first_block + jnp.where(row < slab_blocks, row, row - 2 * slab_blocks)
        gap = query_block - block

        def look(i, chosen):
            return jnp.where(block == vert_ref[h, i], 1, chosen)

        chosen = lax.fori_loop(0, chosen_count, look, filled(shape, 0))
        near = (gap == 0) | ((chosen > 0) & (gap > 0) & (row < slab_blocks))
        bias_ref[h, :2 * slab_blocks] = jnp.where(near | on_slash(gap), 0.0, NEGATIVE)

        shape = (n * CAP, rows)
        row = lax.broadcasted_iota(jnp.int32, shape, 0)
        query_block = first_block + lax.broadcasted_iota(jnp.int32, shape, 1) // BLK

        def extremes(i, found):
            low, high = found
            block = vert_ref[h, i]
            held = row // CAP == block // slab_blocks
            return (jnp.where(held, jnp.minimum(low, block), low),
                    jnp.where(held, jnp.maximum(high, block), high))

        low, high = lax.fori_loop(0, chosen_count, extremes, (filled(shape, none), filled(shape, -1)))
        block = jnp.where(row % CAP == 0, low, jnp.where(high > low, high, none))
        gap = query_block - block
        usable = jnp.where(on_slash(gap), 0, jnp.where(gap > 0, 1, 0))
        bias_ref[h, 2 * slab_blocks:] = jnp.where(usable > 0, 0.0, NEGATIVE)
        return 0

    lax.fori_loop(0, kv, mask_rows, 0)

    def attend(get_k, get_v, bias_row, causal):
        def one_head(h, _):
            k = get_k(h)
            vt = get_v(h).T
            pieces = k.shape[0] // BLK
            heads = [h * per_group + g for g in range(per_group)]
            rows_bias = [bias_ref[h, pl.ds(bias_row + i, 1), :] for i in range(pieces)]
            before = [None if causal else (top[j], total[j]) for j in heads]
            scores = []
            for j in heads:
                q = q_ref[:, pl.ds(pl.multiple_of(j * HEAD_DIM, HEAD_DIM), HEAD_DIM)]
                scores.append(lax.dot_general(k, q, (((1,), (1,)), ((), ())),
                                              preferred_element_type=jnp.float32))
            done = []
            for s, old in zip(scores, before):
                s = s * SCALE
                s = jnp.concatenate(
                    [s[i * BLK:(i + 1) * BLK] + rows_bias[i] for i in range(pieces)], axis=0)
                if causal:
                    keys_at = lax.broadcasted_iota(jnp.int32, s.shape, 0)
                    query_at = lax.broadcasted_iota(jnp.int32, s.shape, 1)
                    s = jnp.where(keys_at <= query_at, s, NEGATIVE)
                peak = jnp.max(s, axis=0, keepdims=True)
                shrink = None
                if not causal:
                    peak = jnp.maximum(old[0], peak)
                    shrink = jnp.exp2(old[0] - peak)
                p = jnp.exp2(s - peak)
                amount = jnp.sum(p, axis=0, keepdims=True)
                if not causal:
                    amount = old[1] * shrink + amount
                mix = jnp.dot(vt, p.astype(jnp.bfloat16), preferred_element_type=jnp.float32)
                done.append((peak, amount, shrink, mix))
            for j, (peak, amount, shrink, mix) in zip(heads, done):
                top[j] = peak
                total[j] = amount
                acc[j] = mix if causal else acc[j] * shrink + mix
            return 0

        lax.fori_loop(0, kv, one_head, 0)

    def lanes(h):
        return pl.ds(pl.multiple_of(h * HEAD_DIM, HEAD_DIM), HEAD_DIM)

    def attend_slots(slab, count):
        def get(first):
            return lambda h: jnp.concatenate(
                [slots[slab + i, first:first + slot_keys, lanes(h)] for i in range(count)], axis=0)

        attend(get(0), get(slot_keys), 2 * slab_blocks + slab * CAP, False)

    attend(lambda h: k_ref[:, lanes(h)], lambda h: v_ref[:, lanes(h)], 0, True)

    for e in range(1, inner):
        peer = (c + inner - e) % inner
        slab = o * inner + peer

        @pl.when((o < outer - 1) | (peer < c))
        def _(slab=slab):
            arrived(slab, 1)

        @pl.when(o < outer - 1)
        def _(slab=slab, e=e):
            relay(slab, 1, v_up.at[0, e], above).start()

    @pl.when(o > 0)
    def _():
        spread_plane(1, True)

    for near in range(inner - 1):
        @pl.when(near < c)
        def _(near=near):
            arrived(o * inner + near, 0)
            attend_slots(o * inner + near, 1)

    @pl.when(me > 0)
    def _():
        for i in range(2):
            remote(prev.at[i], prev.at[i], prev_send.at[i], prev_recv.at[i], above).wait_recv()
        attend(lambda h: prev[0, :, lanes(h)], lambda h: prev[1, :, lanes(h)], slab_blocks, False)

    step = 2 if inner % 2 == 0 else 1

    def plane(d, _):
        @pl.when(d < o)
        def _():
            spread_plane(d + 1, True)

        base = (o - d) * inner
        for part in range(0, inner, step):
            for i in range(part, part + step):
                @pl.when(c != i)
                def _(i=i):
                    arrived(base + i, 0)

            attend_slots(base + part, step)
        return 0

    lax.fori_loop(1, o + 1, plane, 0)

    def finish(j, _):
        a = acc[j] / total[j]
        attn[:, lanes(j)] = a.T.astype(jnp.bfloat16)
        return 0

    lax.fori_loop(0, kv * per_group, finish, 0)
    weight_copy.wait()
    tiles = give.shape[0]
    mine = pl.ds(pl.multiple_of(core * half, half), half)
    theirs = pl.ds(pl.multiple_of(other * half, half), half)

    def swap(t):
        return pltpu.make_async_remote_copy(
            src_ref=give.at[t], dst_ref=take.at[t], send_sem=x_send.at[t], recv_sem=x_recv.at[t],
            device_id=(me, other), device_id_type=MESH,
        )

    def project(t, _):
        columns = pl.ds(pl.multiple_of(t * tile, tile), tile)
        res[t] = jnp.dot(attn[...], w_ref[:, columns], preferred_element_type=jnp.float32)
        give[t] = res[t, theirs, :].astype(jnp.bfloat16)
        swap(t).start()
        return 0

    lax.fori_loop(0, tiles, project, 0)

    def add_up(t, _):
        columns = pl.ds(pl.multiple_of(t * tile, tile), tile)
        swap(t).wait_recv()
        out_ref[:, columns] = (res[t, mine, :] + take[t].astype(jnp.float32)).astype(out_ref.dtype)
        return 0

    lax.fori_loop(0, tiles, add_up, 0)

    def sent(t, _):
        swap(t).wait_send()
        return 0

    lax.fori_loop(0, tiles, sent, 0)
    own_plane(lambda copy: copy.wait_send())
    for e in range(1, inner):
        @pl.when(o < outer - 1)
        def _(e=e):
            relay(o * inner + (c + inner - e) % inner, 1, v_up.at[0, e], above).wait_send()

    def left(d, _):
        spread_plane(d, False)
        return 0

    lax.fori_loop(1, o + 1, left, 0)


def on_device(n, queries, keys, values, vertical, slash, out_weight):
    rows = queries.shape[0]
    kv = vertical.shape[0]
    per_group = queries.shape[1] // (kv * HEAD_DIM)
    slab_blocks = rows // BLK
    inner = math.gcd(n, 4)
    outer = n // inner
    model = out_weight.shape[1]
    cut = CAP * BLK + CAP * BLK // 2

    tile = math.gcd(model, 512)
    tiles = model // tile
    heads = kv * per_group
    vmem = pl.BlockSpec(memory_space=pltpu.VMEM)
    smem = pl.BlockSpec(memory_space=pltpu.SMEM)
    dma = pltpu.SemaphoreType.DMA
    return pl.pallas_call(
        functools.partial(kernel, n, inner, cut, kv, per_group, tile),
        out_shape=jax.ShapeDtypeStruct((rows // 2, model), jnp.bfloat16),
        in_specs=[vmem] * 3 + [smem] * 2 + [pl.BlockSpec(memory_space=pl.ANY)],
        out_specs=vmem,
        scratch_shapes=[
            pltpu.VMEM((2 * CAP * BLK, kv * HEAD_DIM), jnp.bfloat16),
            pltpu.VMEM((kv, 2 * slab_blocks + n * CAP, rows), jnp.float32),
            pltpu.VMEM((n, 2 * CAP * BLK, kv * HEAD_DIM), jnp.bfloat16),
            pltpu.VMEM((2, rows, kv * HEAD_DIM), jnp.bfloat16),
            pltpu.VMEM(out_weight.shape, jnp.bfloat16),
            pltpu.VMEM((heads, HEAD_DIM, rows), jnp.float32),
            pltpu.VMEM((heads, 1, rows), jnp.float32),
            pltpu.VMEM((heads, 1, rows), jnp.float32),
            pltpu.VMEM((rows, heads * HEAD_DIM), jnp.bfloat16),
            pltpu.VMEM((tiles, rows, tile), jnp.float32),
            pltpu.VMEM((tiles, rows // 2, tile), jnp.bfloat16),
            pltpu.VMEM((tiles, rows // 2, tile), jnp.bfloat16),
            dma,
            dma((2,)),
            dma((2,)),
            dma((n, 2)),
            dma((outer,)),
            dma((outer, inner)),
            dma((inner,)),
            dma((outer, inner)),
            dma((tiles,)),
            dma((tiles,)),
        ],
        compiler_params=pltpu.CompilerParams(
            collective_id=0, has_side_effects=True, vmem_limit_bytes=60 * 2**20
        ),
    )(queries, keys, values, vertical, slash, out_weight)


def solution(mesh):
    placed = (
        P("seq", "head"),
        P("seq", "head"),
        P("seq", "head"),
        P("head", None),
        P("head", None),
        P("head", None),
    )
    return jax.shard_map(
        functools.partial(on_device, mesh.shape["seq"]),
        mesh=mesh, in_specs=placed, out_specs=P(("seq", "head"), None), check_vma=False,
    )
```

time: 114 us -> 76.8 us (0.67)
  the two profiles are of different devices: /device:TPU:31 before, /device:TPU:27 now
where the time goes in v2:
time: 76.8 us; the launch traced here: 76.7 us
  Pallas kernels  73 us (95%)
  local copies, waits for them, and re-layouts  3.62 us (5%)
    pallas_call x1, Pallas kernels, on_device(): pl.pallas_call(functools.partial(kernel, n, inner, cut, kv, per_group, ti...  73 us
    unnamed x2, local copies, waits for them, and re-layouts  3.62 us

profile of v2, /device:TPU:27, one launch (start us, length us, event | category | flops | bytes accessed | tf_op | source)
XLA Modules:
  0.0 76.7 jit_solution(3676019508143012557)
XLA Ops:
  0.0 1.3 %copy.7.slash_ref = s32[4,2]{1,0:T(4,128)} copy(s32[4,2]{0,1:T(2,128)} %param.10) | data formatting | bytes 64 | tf_op args[4]
  1.3 73.0 %shard_map.64 = bf16[128,4096]{1,0:T(8,128)(2,1)} custom-call(bf16[256,2048]{1,0:T(8,128)(2,1)} %q_ref.1, bf16[256,512]{1,0:T(8,128)(2,1)} %k_ref.1, bf16[256,512]{1,0:T(8,128)(2,1)} %v_ref.1, s32[4,16]{1,0:T(4,128)} %vert_ref.1, s32[4,2]{1,0:T(4,128)} %copy.7.slash_ref, bf16[2048,4096]{1,0:T(8,128)(2,1)} %w_hbm.1), custom_call_target="tpu_custom_call" | custom-call | tf_op jit(solution)/shard_map/pallas_call | solution.py:360
  74.4 2.3 %copy.9 = bf16[128,4096]{1,0:T(8,128)(2,1)} copy(bf16[128,4096]{1,0:T(8,128)(2,1)} %shard_map.64) | data formatting | bytes 2097152

commit v3 on v2

--- a/solution.py
+++ b/solution.py
@@ -270,7 +270,7 @@
             remote(prev.at[i], prev.at[i], prev_send.at[i], prev_recv.at[i], above).wait_recv()
         attend(lambda h: prev[0, :, lanes(h)], lambda h: prev[1, :, lanes(h)], slab_blocks, False)
 
-    step = 2 if inner % 2 == 0 else 1
+    step = inner
 
     def plane(d, _):
         @pl.when(d < o)
@@ -349,7 +349,7 @@
     inner = math.gcd(n, 4)
     outer = n // inner
     model = out_weight.shape[1]
-    cut = CAP * BLK + CAP * BLK // 2
+    cut = CAP * BLK + CAP * BLK // 8 * 3
 
     tile = math.gcd(model, 512)
     tiles = model // tile

time: 76.8 us -> 74.3 us (0.967)
  Pallas kernels: 73 us -> 70.5 us
    pallas_call x1, Pallas kernels: 73 us -> 70.5 us  [on_device(): pl.pallas_call(functools.partial(kernel, n, inner, cut, kv, per_group, ti...]
where the time goes in v3:
time: 74.3 us; the launch traced here: 74.2 us
  Pallas kernels  70.5 us (95%)
  local copies, waits for them, and re-layouts  3.62 us (5%)
    pallas_call x1, Pallas kernels, on_device(): pl.pallas_call(functools.partial(kernel, n, inner, cut, kv, per_group, ti...  70.5 us
    unnamed x2, local copies, waits for them, and re-layouts  3.62 us

profile of v3, /device:TPU:27, one launch (start us, length us, event | category | flops | bytes accessed | tf_op | source)
XLA Modules:
  0.0 74.2 jit_solution(3054760618303061968)
XLA Ops:
  0.0 1.3 %copy.7.slash_ref = s32[4,2]{1,0:T(4,128)} copy(s32[4,2]{0,1:T(2,128)} %param.10) | data formatting | bytes 64 | tf_op args[4]
  1.3 70.5 %shard_map.64 = bf16[128,4096]{1,0:T(8,128)(2,1)} custom-call(bf16[256,2048]{1,0:T(8,128)(2,1)} %q_ref.1, bf16[256,512]{1,0:T(8,128)(2,1)} %k_ref.1, bf16[256,512]{1,0:T(8,128)(2,1)} %v_ref.1, s32[4,16]{1,0:T(4,128)} %vert_ref.1, s32[4,2]{1,0:T(4,128)} %copy.7.slash_ref, bf16[2048,4096]{1,0:T(8,128)(2,1)} %w_hbm.1), custom_call_target="tpu_custom_call" | custom-call | tf_op jit(solution)/shard_map/pallas_call | solution.py:360
  71.9 2.3 %copy.9 = bf16[128,4096]{1,0:T(8,128)(2,1)} copy(bf16[128,4096]{1,0:T(8,128)(2,1)} %shard_map.64) | data formatting | bytes 2097152
